TPU v7x, 128 devices: a whole 4x4x4 slice. The times are simulated.
128 devices in a mesh: cp: 2 (over core), fsdp: 64 (over z, y, x).
Axes of the slice: x: 4, y: 4, z: 4, core: 2. Of those that a mesh axis runs over, the one named last changes fastest.
Arguments:
- hidden: bfloat16 [64, 1024, 2048], P('fsdp', 'cp')
- tok_pos: int32 [64, 1024], P('fsdp', 'cp')
- grad_out: bfloat16 [64, 1024, 2048], P('fsdp', 'cp')
- norm_gain: float32 [2048], P(('fsdp', 'cp'))
- w_query: bfloat16 [2048, 2048], P(('fsdp', 'cp'))
- w_key: bfloat16 [2048, 256], P(('fsdp', 'cp'))
- w_value: bfloat16 [2048, 256], P(('fsdp', 'cp'))
- w_out: bfloat16 [2048, 2048], P(('fsdp', 'cp'))
Outputs:
- output 1: bfloat16 [64, 1024, 2048], P('fsdp', 'cp')
- output 2: bfloat16 [64, 1024, 2048], P('fsdp', 'cp')
- output 3: float32 [2048, 2048], P(('fsdp', 'cp'))
- output 4: float32 [2048, 256], P(('fsdp', 'cp'))
- output 5: float32 [2048, 256], P(('fsdp', 'cp'))
- output 6: float32 [2048, 2048], P(('fsdp', 'cp'))
- output 7: float32 [2048], P(('fsdp', 'cp'))
All inputs are finite; a program needn't handle non-finite values.
Results may differ from a plain program's by a relative error of at most 0.00684.
Values are sent between devices in bfloat16 or wider.
A program may use at most 1 GiB of HBM per device.

v0:
```python
import functools
import jax
import jax.numpy as jnp
import numpy as np
from jax import lax
from jax.experimental import pallas as pl
from jax.experimental.pallas import tpu as pltpu
from jax.sharding import PartitionSpec as P

LANES, SUBS, RING, TRIO, DUO = 128, 8, 4, 3, 2
PAIR, ROWS, CHIP, SHARE, TURN = 256, 512, 32, 16, 64
HEAD_DIM = LANES
ROPE_THETA = 1000000.0
RMS_EPS = 1e-5
SCALE = HEAD_DIM ** -0.5
LOG2E = 1.4426950408889634

MESH = pl.DeviceIdType.MESH
AXES = ('x', 'y', 'z')
ORDERS = (('x', 'y', 'z'), ('y', 'z', 'x'), ('z', 'x', 'y'))
ALL = pl.ds(0, RING)


def torus():
    f = lax.axis_index('fsdp')
    return {'x': lax.rem(f, RING), 'y': lax.rem(lax.div(f, RING), RING), 'z': lax.div(f, SHARE)}


def step(pos, axis, hop):
    return lax.rem(pos[axis] + hop, RING)


class Batch:
    def __init__(self, comm):
        self.comm, self.index = comm, comm.used
        comm.used += 1

    def _copy(self, src, dst, device):
        send, recv, _ = self.comm.sems
        return pltpu.make_async_remote_copy(src_ref=src, dst_ref=dst, send_sem=send.at[self.index], recv_sem=recv.at[self.index], device_id=device, device_id_type=MESH)

    def send(self, src, dst, device):
        self._copy(src, dst, device).start()
        return self

    def arrived(self, whole):
        self._copy(whole, whole, self.comm.peer()).wait_recv()

    def sent(self, whole):
        self._copy(whole, whole, self.comm.peer()).wait_send()


class Comm:
    def __init__(self, send_sems, recv_sems, local_sems):
        self.pos = torus()
        self.core = lax.axis_index('cp')
        self.sems = (send_sems, recv_sems, local_sems)
        self.used = self.used_local = 0
        self.stored = []

    def far(self, axis, hop):
        p = dict(self.pos)
        p[axis] = step(self.pos, axis, hop)
        return {'fsdp': (p['z'] * RING + p['y']) * RING + p['x'], 'cp': self.core}

    def peer(self):
        return {'fsdp': lax.axis_index('fsdp'), 'cp': 1 - self.core}

    def aside(self, dy, dx):
        return {'fsdp': (self.pos['z'] * RING + step(self.pos, 'y', dy)) * RING + step(self.pos, 'x', dx), 'cp': self.core}

    def announce(self, corners=()):
        sem = pltpu.get_barrier_semaphore()
        for axis in AXES:
            for hop in (1, DUO, TRIO):
                pl.semaphore_signal(sem, inc=1, device_id=self.far(axis, hop), device_id_type=MESH)
        for dy, dx in corners:
            pl.semaphore_signal(sem, inc=1, device_id=self.aside(dy, dx), device_id_type=MESH)
        pl.semaphore_signal(sem, inc=1, device_id=self.peer(), device_id_type=MESH)

    def meet(self, corners=()):
        pl.semaphore_wait(pltpu.get_barrier_semaphore(), 10 + len(corners))

    def ring(self, batch, src, slots, axis):
        for hop in (1, DUO, TRIO):
            batch.send(src, slots.at[hop], self.far(axis, hop))

    def local(self, src, dst):
        i = self.used_local
        self.used_local += 1
        c = pltpu.make_async_copy(src, dst, self.sems[DUO].at[i])
        c.start()
        return c

    def store(self, src, dst):
        self.stored.append(self.local(src, dst))


class Singles(Comm):
    def __init__(self, *sems):
        super().__init__(*sems)
        self.sent, self.exchanged = [], []

    def _copy(self, src, dst, device):
        i = self.used
        self.used += 1
        c = pltpu.make_async_remote_copy(src_ref=src, dst_ref=dst, send_sem=self.sems[0].at[i], recv_sem=self.sems[1].at[i], device_id=device, device_id_type=MESH)
        c.start()
        return c

    def send(self, src, dst, device):
        c = self._copy(src, dst, device)
        self.sent.append(c)
        return c

    def trade(self, src, dst):
        self.exchanged.append(self._copy(src, dst, self.peer()))


def pick(ref, sel, piece):
    lo, cols, first, rows = piece
    return ref.at[sel['z'], sel['y'], sel['x'], pl.ds(first, rows), pl.ds(lo, cols)]


def sem_scratch(remote, local):
    return [pltpu.SemaphoreType.DMA((remote,)), pltpu.SemaphoreType.DMA((remote,)), pltpu.SemaphoreType.DMA((local,))]


def add_into(dst, *srcs, fresh=False):
    def add(idx):
        total, *rest = [s[idx] for s in (srcs if fresh else (dst,) + srcs)]
        for more in rest:
            total = total + more
        dst[idx] = total

    if len(dst.shape) > TRIO:
        @pl.loop(0, dst.shape[0])
        def _(i):
            add((i,))
    else:
        add(Ellipsis)


def halves(lo, n):
    return (lo, n, 0, SHARE), (lo, n, SHARE, SHARE)


GROUPS = (halves(0, 384), halves(384, 384), halves(768, 384))
QK_FIRST = (halves(0, PAIR), halves(384, PAIR), halves(768, PAIR))
QK_LAST = (halves(PAIR, LANES), halves(640, LANES), halves(1024, LANES))
TOKENS = 1024
DIM = 2048
HALF = 1024
QKV = 1280
GROUP = 1152


def scope(name):
    return jax.named_scope(name)


def dot(a, b):
    return jnp.dot(a, b, preferred_element_type=jnp.float32)


def dot_nt(a, b):
    return lax.dot_general(a, b, (((1,), (1,)), ((), ())), preferred_element_type=jnp.float32)


def tile_at(i, n):
    return pl.ds(pl.multiple_of(i * n, n), n)


class Gather:
    def __init__(self, comm, ref, colors, land, held=None):
        self.comm, self.ref, self.colors, self.land = comm, ref, colors, land
        self.held = list(held or [dict(comm.pos) for _ in colors])
        self.spent = []

    def move(self, batch, s, piece, to):
        batch.send(pick(self.ref, s, piece), pick(self.ref, s, piece), to)

    def at(self, k, hop):
        d = ORDERS[k][self.phase]
        return dict(self.held[k], **{d: step(self.comm.pos, d, hop)})

    def begin(self, phase):
        self.phase = phase
        self.rest = Batch(self.comm)
        if phase == 0:
            for hop in (DUO, 1, TRIO):
                for k, (a, _) in enumerate(self.colors):
                    self.move(self.rest, self.held[k], (a[0], a[1], 0, CHIP), self.comm.far(ORDERS[k][0], hop))
            return
        self.up, self.dn = ([Batch(self.comm) for _ in range(TRIO)] for _ in range(DUO))
        for k, (a, b) in enumerate(self.colors):
            d = ORDERS[k][phase]
            up, dn, s = self.comm.far(d, 1), self.comm.far(d, TRIO), self.held[k]
            self.move(self.up[k], s, a, up)
            self.move(self.dn[k], s, b, dn)
            self.move(self.rest, s, b, up)
            self.move(self.rest, s, a, dn)
        if phase == DUO:
            for k, pieces in enumerate(self.colors):
                for piece in pieces:
                    self.land(self.ref, self.held[k], piece)

    def forward(self):
        for k, (a, b) in enumerate(self.colors):
            d = ORDERS[k][self.phase]
            for batch, hop, piece, to in ((self.up[k], TRIO, a, 1), (self.dn[k], 1, b, TRIO)):
                s = self.at(k, hop)
                batch.arrived(pick(self.ref, s, piece))
                self.move(self.rest, s, piece, self.comm.far(d, to))
                if self.phase == DUO:
                    self.land(self.ref, s, piece)
                self.spent.append((batch, pick(self.ref, self.held[k], piece)))

    def end(self):
        axis = ORDERS[0][self.phase]
        blocks = dict(self.held[0], **{axis: pl.ds(0, DUO if self.phase else TRIO)})
        width = sum(a[1] for a, _ in self.colors)
        whole = pick(self.ref, blocks, (0, width, 0, CHIP))
        self.rest.arrived(whole)
        self.spent.append((self.rest, whole))
        for k, (a, b) in enumerate(self.colors):
            if self.phase == DUO:
                for hop, piece in ((TRIO, b), (1, a), (DUO, a), (DUO, b)):
                    self.land(self.ref, self.at(k, hop), piece)
            self.held[k] = dict(self.held[k], **{ORDERS[k][self.phase]: ALL})

    def finish(self):
        for batch, whole in self.spent:
            batch.sent(whole)


def head_kernel(hidden, dy, wq, wk, wv, wo, pos, gain_in, cos_t, sin_t,
                qt_o, dot_o, k_o, kt_o, v_o, vt_o, rt_o, dyc_o, wqk_o, wqkp_o, wvo_o, wvop_o, gain_o,
                hid2, dy2, dys, rs, rt, wqk, wvo, wpeer, pi, pos2, qt, dot_s, kk, kt, vv, vt, cosines, sines, gain, gtile, gbuf, gx, gy, gz, *sems):
    comm = Comm(*sems)
    comm.announce()
    pos_c, core = comm.pos, comm.core
    bf16, f32 = jnp.bfloat16, jnp.float32
    peer = comm.peer()
    rows = tile_at(core, SHARE)
    mine_qk = wqk.at[pos_c['z'], pos_c['y'], pos_c['x'], rows]
    mine_vo = wvo.at[pos_c['z'], pos_c['y'], pos_c['x'], rows]

    def weight_parts(c):
        return ((wq.at[:, tile_at(c, HALF)], mine_qk.at[:, pl.ds(0, HALF)]), (wk.at[:, tile_at(c, LANES)], mine_qk.at[:, pl.ds(HALF, LANES)]),
                (wv.at[:, tile_at(c, LANES)], mine_vo.at[:, pl.ds(0, LANES)]), (wo.at[:, tile_at(c, HALF)], mine_vo.at[:, pl.ds(LANES, HALF)]))

    loads = [comm.local(s, d) for s, d in weight_parts(core)]
    load_x = [comm.local(hidden, hid2.at[pl.ds(0, ROWS)]), comm.local(dy, dy2.at[pl.ds(0, ROWS)])]
    share = lax.broadcasted_iota(jnp.int32, (SUBS, LANES), 1) // SHARE
    gtile[...] = jnp.where(share == pos_c['x'] * DUO + core, jnp.broadcast_to(jnp.concatenate([gain_in[...]] * SUBS, axis=1), (SUBS, LANES)), 0.0)
    with scope('entry'):
        comm.meet()
    swap_w, swap_pos, swap_dy, swap_x, peers_qk, peers_vo = (Batch(comm) for _ in range(6))
    gain_c, gain_x, gain_y, gain_z = (Batch(comm) for _ in range(RING))
    for s, d in weight_parts(1 - core):
        swap_w.send(s, d, peer)
    gain_c.send(gtile, gbuf, peer)
    swap_pos.send(pos, pos2, peer)
    for c in loads:
        c.wait()
    with scope('wait_w'):
        swapped = wqk.at[pos_c['z'], pos_c['y'], pos_c['x']]
        swap_w.arrived(swapped)

    def land_qk(ref, s, cols):
        peers_qk.send(pick(ref, s, cols), pick(wqkp_o, s, cols), peer)

    def land_vo(ref, s, cols):
        peers_vo.send(pick(ref, s, cols), pick(wpeer, s, cols), peer)

    g1 = Gather(comm, wvo, GROUPS, land_vo)
    g2 = Gather(comm, wqk, GROUPS, land_qk)
    g1.begin(0)
    g2.begin(0)
    gain_c.arrived(gbuf)
    gx[0] = gtile[...] + gbuf[...]
    comm.ring(gain_x, gx.at[0], gx, 'x')

    swap_pos.arrived(pos2)

    @pl.loop(0, TOKENS // LANES)
    def _(i):
        want = lax.broadcasted_iota(jnp.int32, (LANES, ROWS), 0) + i * LANES
        for h, have in enumerate((pos, pos2)):
            pi[tile_at(i, LANES), h * ROWS:(h + 1) * ROWS] = jnp.where(want == have[...], 1.0, 0.0).astype(bf16)

    for i in range(RING):
        r = slice(i * PAIR, (i + 1) * PAIR)
        cos, sin = cos_t[:, r], sin_t[:, r]
        cosines[r, :] = jnp.concatenate([cos, cos], axis=0).T
        sines[r, :] = jnp.concatenate([-sin, sin], axis=0).T

    def sort(dst, src, first, last):
        with scope('sort'):
            @pl.loop(first, last)
            def _(j):
                c = tile_at(j, PAIR)
                dst[:, c] = dot(pi[...], src[:, c]).astype(bf16)

    swap_dy.send(dy, dy2.at[pl.ds(ROWS, ROWS)], peer)
    with scope('p0_end'):
        for g in (g1, g2):
            g.end()
            g.begin(1)
    swap_x.send(hidden, hid2.at[pl.ds(ROWS, ROWS)], peer)
    gain_x.arrived(gx.at[pl.ds(1, TRIO)])
    gy[pos_c['y']] = (gx[0] + gx[1]) + (gx[DUO] + gx[TRIO])
    for hop in (1, DUO, TRIO):
        gain_y.send(gy.at[pos_c['y']], gy.at[pos_c['y']], comm.far('y', hop))
    with scope('wait_dy'):
        load_x[1].wait()
        swap_dy.arrived(dy2.at[pl.ds(ROWS, ROWS)])
    sort(dys, dy2, 0, RING)
    with scope('p1a_fwd'):
        g1.forward()
    sort(dys, dy2, RING, 6)
    with scope('p1b_fwd'):
        g2.forward()
    sort(dys, dy2, 6, SUBS)
    with scope('p1a_end'):
        g1.end()
    gain_y.arrived(gy.at[pl.ds(1, TRIO)])
    for j in range(RING):
        gz[pos_c['z'], j] = gy[j]
    for hop in (1, DUO, TRIO):
        gain_z.send(gz.at[pos_c['z']], gz.at[pos_c['z']], comm.far('z', hop))
    g1.begin(DUO)
    comm.store(dys.at[:, tile_at(core, HALF)], dyc_o)
    with scope('p1b_end'):
        g2.end()
    with scope('wait_x'):
        load_x[0].wait()
        swap_x.arrived(hid2.at[pl.ds(ROWS, ROWS)])
    sort(rs, hid2, 0, SUBS)
    with scope('p2q_fwd'):
        g1.forward()
    g2a, g2b = (Gather(comm, wqk, colors, land_qk, g2.held) for colors in (QK_FIRST, QK_LAST))
    g2a.begin(DUO)
    with scope('gain'):
        gain_z.arrived(gz.at[pl.ds(1, TRIO)])
    for i in range(RING):
        for j in range(RING):
            gain[:, (i * RING + j) * LANES:(i * RING + j + 1) * LANES] = gz[i, j]
    comm.store(gain, gain_o)

    def norm(first, last):
        with scope('norm'):
            @pl.loop(first, last)
            def _(i):
                r = tile_at(i, CHIP)
                x = rs[r, :].astype(f32)
                inv = lax.rsqrt(jnp.mean(x * x, axis=-1, keepdims=True) + RMS_EPS)
                rs[r, :] = (x * inv * gain[0:1, :]).astype(bf16)

    norm(0, TOKENS // CHIP)
    with scope('r_t'):
        @pl.loop(0, DIM // PAIR)
        def _(i):
            c = tile_at(i, PAIR)

            @pl.loop(0, TOKENS // PAIR)
            def _(j):
                r = tile_at(j, PAIR)
                rt[c, r] = rs[r, c].T
    comm.store(rt, rt_o)
    with scope('p2o_end'):
        g1.end()
    w_qk, w_vo, w_peer = wqk.reshape(DIM, GROUP), wvo.reshape(DIM, GROUP), wpeer.reshape(DIM, GROUP)
    with scope('vals'):
        @pl.loop(0, DUO)
        def _(i):
            r = tile_at(i, ROWS)
            val = dot(rs[r, :], w_vo[:, :LANES]).astype(bf16)
            vv[r, :] = val
            vt[:, r] = val.T
    for src, dst in ((wvo, wvo_o), (vv, v_o), (vt, vt_o)):
        comm.store(src, dst)
    with scope('p2q_fwd'):
        g2a.forward()
    g2b.begin(DUO)
    with scope('wo_peer'):
        peers_vo.arrived(wpeer)
    comm.store(wpeer, wvop_o)
    with scope('do_t'):
        mine = tile_at(core, HALF)

        @pl.loop(0, TOKENS // PAIR)
        def _(j):
            t = tile_at(j, PAIR)
            w_rows = jnp.concatenate([w_vo[mine, LANES:], w_peer[mine, LANES:]], axis=1)
            d_rows = jnp.concatenate([dys[t, mine], dys[t, tile_at(1 - core, HALF)]], axis=1)
            dot_s[:, t] = dot_nt(w_rows, d_rows).astype(bf16)
    comm.store(dot_s, dot_o)

    def rotated(x, r):
        return (x * cosines[r, :] + pltpu.roll(x, TURN, 1) * sines[r, :]).astype(bf16)

    def queries(columns, heads):
        for i in range(DUO):
            r = slice(i * ROWS, (i + 1) * ROWS)
            x = dot(rs[r, :], columns)
            for h, head in enumerate(heads):
                qt[tile_at(head, LANES), r] = rotated(x[:, h * LANES:(h + 1) * LANES], r).T

    with scope('p2q_end'):
        g2a.end()

    with scope('last_fwd'):
        g2b.forward()
    with scope('q'):
        for t in range(TRIO):
            queries(w_qk[:, t * 384:t * 384 + PAIR], (TRIO * t, TRIO * t + 1))
    for t in range(TRIO):
        two_heads = pl.ds(t * 384, PAIR)
        comm.store(qt.at[two_heads], qt_o.at[two_heads])
    with scope('last_end'):
        g2b.end()
    comm.store(wqk, wqk_o)
    with scope('q_last'):
        last = jnp.concatenate([w_qk[:, PAIR:384], w_qk[:, 640:768], w_qk[:, HALF:]], axis=1)
        for i in range(DUO):
            r = slice(i * ROWS, (i + 1) * ROWS)
            x = dot(rs[r, :], last)
            for h, head in enumerate((DUO, 5)):
                qt[tile_at(head, LANES), r] = rotated(x[:, h * LANES:(h + 1) * LANES], r).T
            key = rotated(x[:, PAIR:], r)
            kk[r, :] = key
            kt[:, r] = key.T
    for src, dst in ((kk, k_o), (kt, kt_o)) + tuple((qt.at[tile_at(h, LANES)], qt_o.at[tile_at(h, LANES)]) for h in (DUO, 5)):
        comm.store(src, dst)
    with scope('finish'):
        peers_qk.arrived(wqk)
        for batch, whole in ((swap_w, swapped), (swap_pos, pos2), (swap_dy, dy2.at[pl.ds(ROWS, ROWS)]), (swap_x, hid2.at[pl.ds(ROWS, ROWS)]), (peers_qk, wqk), (peers_vo, wvo),
                             (gain_c, gbuf), (gain_x, gx.at[pl.ds(1, TRIO)]), (gain_y, gy.at[pl.ds(1, TRIO)]), (gain_z, gz.at[pl.ds(1, TRIO)])):
            batch.sent(whole)
        for g in (g1, g2, g2a, g2b):
            g.finish()
        for c in comm.stored:
            c.wait()


def head(hidden, dy, wq, wk, wv, wo, pos, gain, cos_t, sin_t):
    bf16, f32 = jnp.bfloat16, jnp.float32
    any_ = pl.BlockSpec(memory_space=pl.ANY)
    vmem = pl.BlockSpec(memory_space=pltpu.VMEM)
    S = lambda shape, d=bf16: jax.ShapeDtypeStruct(shape, d)
    V = lambda shape, d=bf16: pltpu.VMEM(shape, d)
    group = (RING, RING, RING, CHIP, GROUP)
    sq, tall, wide = (HALF, TOKENS), (TOKENS, LANES), (LANES, TOKENS)
    full = (TOKENS, DIM)
    return pl.pallas_call(
        head_kernel,
        out_shape=[S(sq), S(sq), S(tall), S(wide), S(tall), S(wide), S((DIM, TOKENS)), S((TOKENS, HALF)), S(group), S(group), S(group), S(group), S((SUBS, DIM), f32)],
        in_specs=[any_] * 6 + [vmem] * RING,
        out_specs=[any_] * 13,
        scratch_shapes=[V(full), V(full), V(full), V(full), V((DIM, TOKENS)), V(group), V(group), V(group), V((TOKENS, TOKENS)), V((1, ROWS), jnp.int32),
                        V(sq), V(sq), V(tall), V(wide), V(tall), V(wide), V(tall, f32), V(tall, f32), V((SUBS, DIM), f32), V((SUBS, LANES), f32), V((SUBS, LANES), f32), V((RING, SUBS, LANES), f32), V((RING, SUBS, LANES), f32), V((RING, RING, SUBS, LANES), f32)] + sem_scratch(47, 22),
        compiler_params=pltpu.CompilerParams(collective_id=0, has_side_effects=True, vmem_limit_bytes=60 * DUO**20),
        name='head',
    )(hidden, dy, wq, wk, wv, wo, pos, gain, cos_t, sin_t)


HEADS = SUBS
UNIT_K, UNIT_V = SUBS, 9
N_UNITS = 18
GAIN = N_UNITS
SLOTS = RING
LAST = 5
ABREAST = DUO
LINES = ((0, TRIO, 6, 9, 12, 15), (1, RING, 7, 10, 13, SHARE), (DUO, 5, SUBS, 11, 14, 17))
COLOR = {u: k for k, line in enumerate(LINES) for u in line}
RANK = {u: i for line in LINES for i, u in enumerate(line)}
SWAPPED = (1, TRIO, RING, SUBS, 10)
ORDER = {u: ORDERS[k] if u not in SWAPPED else (ORDERS[k][0], ORDERS[k][DUO], ORDERS[k][1]) for u, k in COLOR.items()}
BEFORE = {u: line[i - SLOTS] if i >= SLOTS else None for line in LINES for i, u in enumerate(line)}
PLACES = 12
PLACE = {u: u % PLACES for u in range(N_UNITS)}
WIRE = (2.82, 0.71, 0.36)
LATENCY = 2.4
STAGE_COST = 0.08


class Plan:
    def __init__(self):
        self.now, self.stage, self.ready, self.order, self.link = 0.0, {}, {}, [], {}
        self.mark = {}

    def _wire(self, u, phase, count):
        link = ORDER[u][phase]
        t = max(self.link.get(link, 0.0), self.now)
        first = t + WIRE[phase] + LATENCY
        self.link[link] = t + WIRE[phase] * count
        return first if phase < DUO else self.link[link] + LATENCY

    def free(self, u, phase):
        if BEFORE[u] is None:
            return True
        done = self.mark.get((BEFORE[u], (DUO, RING, 5)[phase]))
        if done is None:
            return False
        sent = ((0, 1), (DUO, TRIO), (RING,))[phase]
        return any(self.mark.get((j, s), -1) > done and (j, s + 1) in self.mark for j, order in ORDER.items() if order[phase] == ORDER[u][phase] for s in sent)

    def run(self, u):
        stage = self.stage[u]
        self.order.append((u, stage))
        self.mark[u, stage] = len(self.order)
        self.now = max(self.now, self.ready[u]) + STAGE_COST
        self.stage[u] = stage + 1
        if stage == (TRIO if u == GAIN else LAST):
            del self.stage[u]
        elif u == GAIN:
            self.ready[u] = max([self.now] + [self.link.get(a, 0.0) for a in ('', 'z', 'xy')[stage]]) + DUO * LATENCY
        elif stage % DUO:
            self.ready[u] = self._wire(u, stage // DUO, 1)
        else:
            self.ready[u] = self._wire(u, stage // DUO, DUO)

    def blocked(self, u):
        stage = self.stage[u]
        if u == GAIN:
            return False
        if stage == 0 and sum(0 < self.stage.get(j, 0) <= DUO for j in LINES[COLOR[u]]) >= ABREAST:
            return True
        if stage == DUO and BEFORE[u] is not None and (BEFORE[u], LAST) not in self.mark:
            return True
        return stage in (0, DUO, RING) and not self.free(u, stage // DUO)

    def start(self, u):
        self.stage[u], self.ready[u] = 0, self.now

    def due(self):
        first = len(self.order)
        while True:
            ripe = [(self.ready[u], u) for u in self.stage if self.ready[u] <= self.now and not self.blocked(u)]
            if not ripe:
                return self.order[first:]
            self.run(min(ripe)[1])

    def vacated(self, u):
        return (u, DUO) in self.mark

    def rush(self, done):
        first = len(self.order)
        while not done():
            self.run(min((self.ready[u], u) for u in self.stage if not self.blocked(u))[1])
        return self.order[first:]


QB = PAIR
PAIRS = HEADS // DUO
NBLK = TOKENS // QB
HALVES = (pl.ds(0, SHARE), pl.ds(SHARE, SHARE))
PLANE = tuple((dy, dx) for dy in range(RING) for dx in range(RING) if dy or dx)
CORNERS = tuple((dy, dx) for dy, dx in PLANE if dy and dx)


class Scatter:
    def __init__(self, comm, part, mid, bufs, fin, outs, send_sems, recv_sems, swap_sems):
        self.pos, self.part, self.mid, self.bufs, self.fin, self.outs = comm.pos, part, mid, bufs, fin, outs
        self.send_sems, self.recv_sems, self.swap_sems = send_sems, recv_sems, swap_sems
        self.near = {(a, hop): comm.far(a, hop) for a in AXES for hop in (1, DUO, TRIO)}
        self.hops = {(a, hop): step(comm.pos, a, hop) for a in AXES for hop in (1, DUO, TRIO)}
        self.peer, self.core = comm.peer(), comm.core
        self.keep, self.give = tile_at(comm.core, SHARE), tile_at(1 - comm.core, SHARE)
        self.drained = set()

    def slot(self, u):
        return COLOR[u], RANK[u] % SLOTS

    def buf(self, u, phase):
        return self.bufs[phase].at[self.slot(u)]

    def view(self, u, phase, hop, half=None):
        order = ORDER[u]
        at = {a: ALL for a in AXES}
        for a in order[1:phase]:
            at[a] = self.pos[a]
        at[order[phase]] = self.hops[order[phase], hop] if hop else self.pos[order[phase]]
        rows = pl.ds(0, CHIP) if half is None else HALVES[half]
        if phase == 0:
            return self.part.at[PLACE[u], at['z'], at['y'], at['x'], rows, :]
        return self.mid.at[self.slot(u) + tuple(at[a] for a in 'zyx' if a != order[0]) + (rows, slice(None))]

    def copy(self, src, dst, sems, device):
        return pltpu.make_async_remote_copy(src_ref=src, dst_ref=dst, send_sem=sems[0], recv_sem=sems[1], device_id=device, device_id_type=MESH)

    def sems(self, u, phase, kind=0):
        k, i = self.slot(u)
        at = (k * SLOTS + i) * TRIO + phase
        return self.send_sems.at[at], self.recv_sems.at[(k * SLOTS + i) * 5 + DUO * phase + kind]

    def send(self, u, phase, name):
        axis = ORDER[u][phase]
        if phase == DUO:
            src, to = self.view(u, DUO, name + 1), name + 1
        else:
            hop, half, to = ((DUO, 0, 1), (DUO, 1, TRIO), (1, 1, 1), (TRIO, 0, TRIO), (1, 0, 1), (TRIO, 1, TRIO))[name]
            src = self.view(u, phase, hop, half)
        self.copy(src, self.buf(u, phase).at[name], self.sems(u, phase, int(name > 1 and phase < DUO)), self.near[axis, to]).start()

    def launch(self, u, phase):
        if BEFORE[u] is not None:
            self.drain(BEFORE[u], phase)
        for name in range(RING if phase < DUO else TRIO):
            self.send(u, phase, name)

    def arrived(self, u, phase, first, count):
        whole = self.buf(u, phase).at[pl.ds(first, count)]
        self.copy(whole, whole, self.sems(u, phase, int(first > 0)), self.peer).wait_recv()

    def drain(self, u, phase):
        if (u, phase) not in self.drained:
            self.drained.add((u, phase))
            whole = self.buf(u, phase)
            self.copy(whole, whole, self.sems(u, phase), self.peer).wait_send()

    def out(self, u):
        if u < HEADS:
            out, col = self.outs[0], self.core * HALF + u * LANES
        elif u < 10:
            out, col = self.outs[u - 7], self.core * LANES
        else:
            out, col = self.outs[TRIO], self.core * HALF + (u - 10) * LANES
        return out.at[:, pl.ds(pl.multiple_of(col, LANES), LANES)]

    def kept(self, u):
        return pltpu.make_async_copy(self.fin.at[u, self.keep], self.out(u), self.swap_sems.at[DUO + u])

    def run(self, u, stage):
        if stage == 0:
            return self.launch(u, 0)
        phase = (stage - 1) // DUO
        if stage == LAST:
            self.arrived(u, DUO, 0, TRIO)
            got = self.buf(u, DUO)
            self.fin[u] = self.view(u, DUO, 0)[...] + (got[0] + got[1] + got[DUO])
            self.copy(self.fin.at[u, self.give], self.out(u), (self.swap_sems.at[0], self.swap_sems.at[1]), self.peer).start()
            self.kept(u).start()
            return
        got = self.buf(u, phase)
        if stage % DUO:
            self.arrived(u, phase, 0, DUO)
            for name, hop in ((0, 1), (1, TRIO)):
                add_into(self.view(u, phase, hop, name), got.at[name])
                self.send(u, phase, name + RING)
            return
        self.arrived(u, phase, DUO, RING)
        if phase == 0 and BEFORE[u] is not None:
            self.drain(BEFORE[u], 1)
            self.drain(BEFORE[u], DUO)
        for half, names in ((0, (TRIO, RING)), (1, (DUO, 5))):
            if phase:
                add_into(self.view(u, phase, 0, half), *[got.at[name] for name in names])
            else:
                dst = self.mid.at[self.slot(u) + (ALL, ALL, HALVES[half], slice(None))]
                add_into(dst, self.view(u, 0, 0, half), *[got.at[name] for name in names], fresh=True)
        self.launch(u, phase + 1)

    def finish(self):
        for u in range(N_UNITS):
            for phase in range(TRIO):
                self.drain(u, phase)
        half = self.fin.at[:, pl.ds(0, SHARE)]
        swaps = self.copy(half, half, (self.swap_sems.at[0], self.swap_sems.at[1]), self.peer)
        swaps.wait_send()
        swaps.wait_recv()
        for u in range(N_UNITS):
            self.kept(u).wait()


def attend(heads, qt, do_t, k, kt, v, vt, cos, sin, o_row, ot, dq, dkt, dvt, s_scr, e_scr, p_scr, d_scr):
    f32, bf16 = jnp.float32, jnp.bfloat16
    strip = TURN
    work = [(h, j) for j in range(NBLK) for h in range(len(heads))]

    def strips(c):
        return [(i * strip, slice(c * QB + i * strip, c * QB + (i + 1) * strip)) for i in range(QB // strip)]

    def fold(x, op):
        return op(x.reshape(strip // SUBS, SUBS, QB), axis=0)

    def scores(i):
        (h, j), b = work[i], i % DUO
        q_t = qt[heads[h], j * QB:(j + 1) * QB]
        top = jnp.full((SUBS, QB), -jnp.inf, f32)
        for c in range(j + 1):
            tile = dot(k[c * QB:(c + 1) * QB, :], q_t)
            for at, rows in strips(c):
                s = tile[at:at + strip]
                if c == j:
                    seen = lax.broadcasted_iota(jnp.int32, (strip, QB), 0) + at <= lax.broadcasted_iota(jnp.int32, (strip, QB), 1)
                    s = jnp.where(seen, s, -jnp.inf)
                s_scr[b, rows, :] = s
                top = jnp.maximum(top, fold(s, jnp.max))
        return jnp.max(top, axis=0, keepdims=True)

    def rest(i, m):
        (h, j), b = work[i], i % DUO
        cols, n = slice(j * QB, (j + 1) * QB), (j + 1) * QB
        q_t, d_t = qt[heads[h], cols], do_t[heads[h], cols]
        tot = jnp.zeros((SUBS, QB), f32)
        for c in range(j + 1):
            for at, rows in strips(c):
                e = jnp.exp2((s_scr[b, rows, :] - m) * (SCALE * LOG2E))
                s_scr[b, rows, :] = e
                e_scr[b, rows, :] = e.astype(bf16)
                tot = tot + fold(e, jnp.sum)
        den = jnp.sum(tot, axis=0, keepdims=True)
        inv = 1.0 / den
        o = (dot(vt[:, :n], e_scr[b, :n, :]) / den).astype(bf16)
        ot[o_row(h), cols] = o
        delta = jnp.sum(d_t.astype(f32) * o.astype(f32), axis=0, keepdims=True)
        for c in range(j + 1):
            dp = dot(v[c * QB:(c + 1) * QB, :], d_t)
            for at, rows in strips(c):
                p = s_scr[b, rows, :] * inv
                p_scr[b, rows, :] = p.astype(bf16)
                d_scr[b, rows, :] = (p * (dp[at:at + strip] - delta)).astype(bf16)
        dvt[:, :n] += dot_nt(d_t, p_scr[b, :n, :])
        dkt[:, :n] += dot_nt(q_t, d_scr[b, :n, :])
        g = dot(kt[:, :n], d_scr[b, :n, :]) * SCALE
        co, si = cos[:, cols], sin[:, cols]
        x, y = g[:TURN], g[TURN:]
        dq[heads[h], cols] = jnp.concatenate([x * co + y * si, y * co - x * si], axis=0).astype(bf16)

    m = scores(0)
    for i in range(len(work)):
        later = scores(i + 1) if i + 1 < len(work) else None
        rest(i, m)
        m = later


def tail_kernel(qt, do_t, k, kt, v, vt, rt, dyc, wqk, wqkp, wvo, wvop, gain, hidden, dy, pos, cos, sin,
                result, grad_x, gq, gk, gv, go, gout,
                two, ks, kts, vs, vts, rts, ots, dqo, dqp, dkvo, dkvp, dkt, dvt, s_scr, e_scr, p_scr, d_scr, dycs, part, mid, buf1, buf2, buf3, fin, own, onat, dnat, xs, gacc, gpart, gpeer, gz, gx,
                send_sems, recv_sems, swap_sems, trade_send, trade_recv, local_sems):
    comm = Singles(trade_send, trade_recv, local_sems)
    comm.used = HEADS
    f32, bf16 = jnp.float32, jnp.bfloat16
    core, peer = comm.core, comm.peer()
    a1, a2 = two.at[0], two.at[1]
    sc = Scatter(comm, part, mid, (buf1, buf2, buf3), fin, (gq, gk, gv, go), send_sems, recv_sems, swap_sems)
    plan = Plan()
    some, most = pl.ds(0, PAIR), pl.ds(PAIR, HALF - PAIR)
    loads = [comm.local(s, d) for s, d in ((qt.at[some], two.at[0, some]), (k, ks), (do_t.at[some], two.at[1, some]), (vt, vts), (v, vs), (kt, kts))]
    comm.announce(CORNERS)
    dkt[...] = jnp.zeros_like(dkt)
    dvt[...] = jnp.zeros_like(dvt)
    with scope('wait_q'):
        for c in loads:
            c.wait()
    loads = [comm.local(s, d) for s, d in ((rt, rts), (qt.at[most], two.at[0, most]), (do_t.at[most], two.at[1, most]))]
    later = [comm.local(s, d) for s, d in ((dyc, dycs), (hidden, xs))]

    def emit(stages):
        for u, stage in stages:
            with scope(f'u{u}_s{stage}'):
                if u == GAIN:
                    sum_gain(stage)
                else:
                    sc.run(u, stage)

    def after(cost):
        plan.now += cost
        return plan.due()

    def head_trades(g):
        row = pl.ds(pl.multiple_of((core * HEADS + DUO * g) * LANES, PAIR), PAIR)
        mine = tile_at(g, PAIR)
        return [pltpu.make_async_remote_copy(src_ref=s, dst_ref=d, send_sem=trade_send.at[i], recv_sem=trade_recv.at[i], device_id=peer, device_id_type=MESH)
                for s, d, i in ((ots.at[row], ots.at[row], g), (dqo.at[mine], dqp.at[mine], PAIRS + g))]

    def gradient(place, count, left, right, mul):
        with scope('grad'):
            @pl.loop(0, DUO)
            def _(z):
                g = mul(left[tile_at(z, HALF), :], right())
                for i in range(count):
                    part[place + i, tile_at(z, DUO)] = g[:, i * LANES:(i + 1) * LANES].reshape(DUO, RING, RING, CHIP, LANES)

    attended, paired = [], []
    for g in range(PAIRS):
        attended.append(after(5.1))
        plan.now += 1.5
        plan.start(DUO * g)
        plan.start(DUO * g + 1)
        paired.append(plan.due())

    @pl.loop(0, PAIRS)
    def _(g):
        def at(table):
            for i in range(PAIRS):
                if table[i]:
                    pl.when(g == i)(functools.partial(emit, table[i]))

        heads = [tile_at(DUO * g + i, LANES) for i in range(DUO)]
        with scope('attend'):
            attend(heads, a1, a2, ks, kts, vs, vts, cos, sin, lambda i: tile_at(core * HEADS + DUO * g + i, LANES), ots, dqo, dkt, dvt, s_scr, e_scr, p_scr, d_scr)

        @pl.when(g == 0)
        def _():
            with scope('entry'):
                comm.meet(CORNERS)
                for c in loads:
                    c.wait()
        for c in head_trades(g):
            c.start()
        at(attended)
        gradient(DUO * g, DUO, rts, lambda: dqo[tile_at(g, PAIR), :], dot_nt)
        at(paired)

    def beat(cost, *starts):
        plan.now += cost
        for u in starts:
            plan.start(u)
        emit(plan.due())

    wkv, wkvp = e_scr.reshape(DIM, PAIR), p_scr.reshape(DIM, PAIR)
    later += [comm.local(src.at[:, pl.ds(at, LANES)], dst.at[:, pl.ds(to, LANES)]) for srcs, dst in (((wqk, wvo), wkv), ((wqkp, wvop), wkvp)) for src, at, to in ((srcs[0], HALF, 0), (srcs[1], 0, LANES))]
    wqp_loads = [comm.local(wqkp.at[tile_at(i, HALF), pl.ds(0, HALF)], two.at[i]) for i in range(DUO)]
    key = dkt[...] * SCALE
    co, si, x, y = cos[...], sin[...], key[:TURN], key[TURN:]
    dkvo[:LANES, :] = jnp.concatenate([x * co + y * si, y * co - x * si], axis=0).astype(bf16)
    dkvo[LANES:, :] = dvt[...].astype(bf16)
    comm.trade(dkvo, dkvp)
    gradient(UNIT_K, DUO, rts, lambda: dkvo[...], dot_nt)
    beat(1.8, UNIT_K, UNIT_V)
    wq_load = comm.local(wqk.at[:, pl.ds(0, HALF)], rts)
    for c in later:
        c.wait()
    with scope('trades'):
        for g in range(PAIRS):
            for c in head_trades(g):
                c.wait()

    waiting = list(range(RING))

    def output_gradients(force=False):
        while waiting:
            first = 10 + DUO * waiting[0]
            before = [u for u in range(N_UNITS) if u < first and PLACE[u] in (PLACE[first], PLACE[first + 1])]
            if force:
                emit(plan.rush(lambda: all(map(plan.vacated, before))))
            if not all(map(plan.vacated, before)):
                return
            for u in before:
                sc.drain(u, 0)
            i = waiting.pop(0)
            gradient(PLACE[first], DUO, ots, lambda: dycs[:, i * PAIR:(i + 1) * PAIR], dot)
            plan.start(first)
            plan.start(first + 1)
            beat(1.5)

    def piece(cost):
        beat(cost)
        output_gradients()

    def ticking(n, cost, body):
        tables = [after(cost) for _ in range(n)]

        @pl.loop(0, n)
        def _(i):
            body(i)
            for j, table in enumerate(tables):
                if table:
                    pl.when(i == j)(functools.partial(emit, table))
        output_gradients()

    @pl.loop(0, TOKENS // LANES)
    def _(i):
        want = lax.broadcasted_iota(jnp.int32, (LANES, ROWS), 0) + i * LANES
        own[tile_at(i, LANES), :] = jnp.where(want == pos[...], 1.0, 0.0).astype(bf16)

    def unsort(at, src_t, n):
        with scope('unsort'):
            dnat[at:at + n, :] = dot(src_t[:n, :], own[...]).astype(bf16)

    output_gradients()
    for c in comm.exchanged:
        c.wait_recv()
    unsort(0, dqo, HALF)
    dy_loads = [comm.local(dy.at[:, tile_at(i, HALF)], dqo.at[tile_at(i, ROWS)]) for i in range(DUO)]
    piece(1.2)
    unsort(HALF, dqp, HALF)
    piece(1.2)
    unsort(DUO * HALF, dkvo, PAIR)
    unsort(DUO * HALF + PAIR, dkvp, PAIR)
    piece(0.7)
    wq_load.wait()
    for c in wqp_loads + dy_loads:
        c.wait()
    gacc[...] = jnp.zeros_like(gacc)

    def dr_parts(half, r):
        return [s_scr.at[half, r(i * PAIR), :] for i in range(RING)]

    def back(block, then):
        def dr(half):
            with scope('dr'):
                c = tile_at(half, HALF)
                left = jnp.concatenate([rts[c, :], two[half], wkv[c, :], wkvp[c, :]], axis=1)
                acc = dot(left, dnat[:, block * PAIR:(block + 1) * PAIR])
                for i, ref in enumerate(dr_parts(half, lambda at: pl.ds(at, PAIR))):
                    ref[...] = acc[i * PAIR:(i + 1) * PAIR, :].T

        def norm(part):
            with scope('back'):
                @pl.loop(0, RING)
                def _(i):
                    j = part * RING + i
                    q = pl.ds(pl.multiple_of(block * PAIR + j * SHARE, SHARE), SHARE)
                    d = jnp.concatenate([ref[...] for half in range(DUO) for ref in dr_parts(half, lambda at: pl.ds(pl.multiple_of(at + j * SHARE, SHARE), SHARE))], axis=1)
                    x = xs[q, :].astype(f32)
                    inv = lax.rsqrt(jnp.mean(x * x, axis=-1, keepdims=True) + RMS_EPS)
                    unit = x * inv
                    gacc[...] += jnp.sum((d * unit).reshape(DUO, SUBS, DIM), axis=0)
                    dg = d * gain[0:1, :]
                    new = inv * (dg - unit * jnp.mean(dg * unit, axis=-1, keepdims=True))
                    for half in range(DUO):
                        r = pl.ds(pl.multiple_of(half * ROWS + block * PAIR + j * SHARE, SHARE), SHARE)
                        dqo[r, :] = (dqo[r, :].astype(f32) + new[:, half * HALF:(half + 1) * HALF]).astype(bf16)

        ticking(DUO, 1.6, dr)
        then()
        ticking(RING, 0.92, norm)

    back(0, lambda: None)
    wo_loads = []
    back(1, lambda: wo_loads.extend([comm.local(wvo.at[:, pl.ds(LANES, HALF)], rts)] + [comm.local(wvop.at[tile_at(i, HALF), pl.ds(LANES, HALF)], two.at[i]) for i in range(DUO)]))
    for i in range(DUO):
        comm.store(dqo.at[tile_at(i, ROWS)], grad_x.at[:, tile_at(i, HALF)])
    total = jnp.sum(gacc[...], axis=0, keepdims=True)
    gpart[...] = jnp.zeros_like(gpart)
    for i in range(RING):
        for j in range(RING):
            gpart[i, j:j + 1, :] = total[:, (i * RING + j) * LANES:(i * RING + j + 1) * LANES]

    gain_c, gain_z, gain_p = (Batch(comm) for _ in range(TRIO))

    def sum_gain(stage):
        if stage == 0:
            gain_c.send(gpart, gpeer, peer)
        elif stage == 1:
            gain_c.arrived(gpeer)
            for j in range(RING):
                gz[j] = gpart[j] + gpeer[j]
            for hop in (1, DUO, TRIO):
                gain_z.send(gz.at[step(comm.pos, 'z', hop)], gz.at[TRIO + hop], comm.far('z', hop))
        elif stage == DUO:
            gain_z.arrived(gz.at[pl.ds(RING, TRIO)])
            gx[0] = (gz[comm.pos['z']] + gz[RING]) + (gz[5] + gz[6])
            for dy, dx in PLANE:
                gain_p.send(gx.at[0], gx.at[dy * RING + dx], comm.aside(dy, dx))
        else:
            gain_p.arrived(gx.at[pl.ds(1, 15)])
            gpeer[0] = jnp.sum(gx[...], axis=0)
            mine = jnp.broadcast_to(gpeer[0, pl.ds(comm.pos['y'], 1), :], (SUBS, LANES))
            gout[...] = pltpu.roll(mine, LANES - (comm.pos['x'] * CHIP + core * SHARE), 1)

    plan.start(GAIN)
    beat(0.2)
    for i in range(DUO):
        with scope('unsort_o'):
            @pl.loop(0, DUO)
            def _(j):
                r = pl.ds(pl.multiple_of(i * HALF + j * ROWS, ROWS), ROWS)
                onat[:, r] = dot(ots[r, :], own[...]).astype(bf16).T
        piece(1.58)
    output_gradients(True)

    def project_out(col, weights, i):
        with scope('project'):
            @pl.loop(DUO * i, DUO * i + DUO)
            def _(j):
                c = tile_at(j, PAIR)
                dst = pl.ds(pl.multiple_of(col + j * PAIR, PAIR), PAIR)
                xs[:, dst] = (xs[:, dst].astype(f32) + dot(onat[...], weights(c))).astype(bf16)
        beat(1.48)

    def own_half(c):
        return rts[:, c]

    def other_half(c):
        return jnp.concatenate([a1[:, c], a2[:, c]], axis=0)

    for c in wo_loads:
        c.wait()
    for col, weights in ((core * HALF, own_half), ((1 - core) * HALF, other_half)):
        for i in range(DUO):
            project_out(col, weights, i)
    comm.store(xs, result)
    emit(plan.rush(lambda: not plan.stage))
    with scope('finish'):
        sc.finish()
        for batch, whole in ((gain_c, gpart), (gain_z, gz.at[pl.ds(RING, TRIO)]), (gain_p, gx.at[pl.ds(1, 15)])):
            batch.sent(whole)
        for c in comm.exchanged:
            c.wait_send()
        for c in comm.stored:
            c.wait()


def tail(qt, do_t, k, kt, v, vt, rt, dyc, wqk, wqkp, wvo, wvop, gain, hidden, dy, pos, cos, sin):
    bf16, f32 = jnp.bfloat16, jnp.float32
    any_ = pl.BlockSpec(memory_space=pl.ANY)
    vmem = pl.BlockSpec(memory_space=pltpu.VMEM)
    S = lambda shape, d=bf16: jax.ShapeDtypeStruct(shape, d)
    V = lambda shape, d=bf16: pltpu.VMEM(shape, d)
    D = lambda n: pltpu.SemaphoreType.DMA((n,))
    sq, tall, wide = (HALF, TOKENS), (TOKENS, LANES), (LANES, TOKENS)
    mine, kv = (ROWS, DIM), (PAIR, TOKENS)
    return pl.pallas_call(
        tail_kernel,
        out_shape=[S(mine), S(mine), S((SHARE, DIM), f32), S((SHARE, PAIR), f32), S((SHARE, PAIR), f32), S((SHARE, DIM), f32), S((SUBS, LANES), f32)],
        in_specs=[any_] * 12 + [vmem] + [any_] * DUO + [vmem] * TRIO,
        out_specs=[any_] * 6 + [vmem],
        scratch_shapes=[V((DUO,) + sq), V(tall), V(wide), V(tall), V(wide), V((DIM, TOKENS)), V((DIM, TOKENS)), V(sq), V(sq), V(kv), V(kv), V(wide, f32), V(wide, f32),
                        V((DUO, TOKENS, QB), f32), V((DUO, TOKENS, QB)), V((DUO, TOKENS, QB)), V((DUO, TOKENS, QB)), V(sq), V((PLACES, RING, RING, RING, CHIP, LANES), f32), V((TRIO, SLOTS, RING, RING, CHIP, LANES), f32),
                        V((TRIO, SLOTS, 6, RING, RING, SHARE, LANES), f32), V((TRIO, SLOTS, 6, RING, SHARE, LANES), f32), V((TRIO, SLOTS, TRIO, CHIP, LANES), f32), V((N_UNITS, CHIP, LANES), f32), V((TOKENS, ROWS)), V(mine), V((DUO * QKV, ROWS)), V(mine),
                        V((SUBS, DIM), f32), V((RING, SUBS, LANES), f32), V((RING, SUBS, LANES), f32), V((7, SUBS, LANES), f32), V((SHARE, SUBS, LANES), f32),
                        D(9 * SLOTS), D(15 * SLOTS), D(DUO + N_UNITS), D(HEADS + RING), D(HEADS + RING), D(26)],
        compiler_params=pltpu.CompilerParams(collective_id=1, has_side_effects=True, vmem_limit_bytes=67043328),
        name='tail',
    )(qt, do_t, k, kt, v, vt, rt, dyc, wqk, wqkp, wvo, wvop, gain, hidden, dy, pos, cos, sin)


def settle_kernel(n, *refs):
    ins, gain, outs, gain_out, bufs, sems = refs[:n], refs[n], refs[n + 1:DUO * n + 1], refs[DUO * n + 1], refs[DUO * n + DUO:-1], refs[-1]
    jobs = []
    for a, o, b in zip(ins, outs, bufs):
        size = a.shape[0] // RING if a.shape[0] == ROWS else a.shape[0]
        jobs += [tuple(r.at[pl.ds(i, size)] for r in (a, b, o)) for i in range(0, a.shape[0], size)]
    takes = [pltpu.make_async_copy(a, b, sems.at[0, i]) for i, (a, b, _) in enumerate(jobs)]
    puts = [pltpu.make_async_copy(b, o, sems.at[1, i]) for i, (_, b, o) in enumerate(jobs)]
    for c in takes:
        c.start()
    gain_out[...] = gain[0:1, :SHARE]
    for take, put in zip(takes, puts):
        take.wait()
        put.start()
    for c in puts:
        c.wait()


def settle(*arrays):
    *large, gain = arrays
    any_, vmem = pl.BlockSpec(memory_space=pl.ANY), pl.BlockSpec(memory_space=pltpu.VMEM)
    return pl.pallas_call(
        functools.partial(settle_kernel, len(large)),
        out_shape=[jax.ShapeDtypeStruct(a.shape, a.dtype) for a in large] + [jax.ShapeDtypeStruct((1, SHARE), gain.dtype)],
        in_specs=[any_] * len(large) + [vmem],
        out_specs=[any_] * len(large) + [vmem],
        scratch_shapes=[pltpu.VMEM(a.shape, a.dtype) for a in large] + [pltpu.SemaphoreType.DMA((DUO, 12))],
        name='settle',
    )(*arrays)


def rope_tables():
    j = np.arange(HEAD_DIM // DUO, dtype=np.float64) / (HEAD_DIM // DUO)
    freq = (ROPE_THETA ** -j).astype(np.float32)
    angle = freq[:, None] * np.arange(TOKENS, dtype=np.float32)[None, :]
    return np.cos(angle.astype(np.float64)).astype(np.float32), np.sin(angle.astype(np.float64)).astype(np.float32)


def solution(mesh):
    def shard_fn(hidden, tok_pos, grad_out, norm_gain, w_query, w_key, w_value, w_out):
        hidden, grad_out = hidden[0], grad_out[0]
        cos_t, sin_t = (jnp.asarray(t) for t in rope_tables())
        *parts, gain = head(hidden, grad_out, w_query, w_key, w_value, w_out, tok_pos, norm_gain.reshape(1, SHARE), cos_t, sin_t)
        parts = [p.reshape(DIM, GROUP) if p.ndim > DUO else p for p in parts]
        result, grad_hidden, gq, gk, gv, go, gout = settle(*tail(*parts, gain, hidden, grad_out, tok_pos, cos_t, sin_t))
        return result[None], grad_hidden[None], gq, gk, gv, go, gout.reshape(SHARE)

    row_spec, pos_spec = P('fsdp', 'cp', None), P('fsdp', 'cp')
    weight_spec, gain_spec = P(('fsdp', 'cp'), None), P(('fsdp', 'cp'))
    return jax.shard_map(shard_fn, mesh=mesh, in_specs=(row_spec, pos_spec, row_spec, gain_spec, weight_spec, weight_spec, weight_spec, weight_spec), out_specs=(row_spec, row_spec, weight_spec, weight_spec, weight_spec, weight_spec, gain_spec), check_vma=False)
```

profile of v0, /device:TPU:1, one launch (start us, length us, event | category | flops | bytes accessed | tf_op | source)
XLA Modules:
  0.0 157.3 jit_solution(449935009794224348)
XLA Ops:
  0.6 56.5 %head.1 = (bf16[1024,1024]{1,0:T(8,128)(2,1)}, bf16[1024,1024]{1,0:T(8,128)(2,1)}, bf16[1024,128]{1,0:T(8,128)(2,1)}, bf16[128,1024]{1,0:T(8,128)(2,1)}, bf16[10...) custom-call(bf16[512,2048]{1,0:T(8,128)(2,1)} %bitcast.10, ...), custom_call_target="tpu_custom_call" | custom-call | tf_op jit(solution)/shard_map/head/pallas_call | solution.py:457
  57.1 95.0 %tail.1 = (bf16[512,2048]{1,0:T(8,128)(2,1)}, bf16[512,2048]{1,0:T(8,128)(2,1)}, f32[16,2048]{1,0:T(8,128)}, f32[16,256]{1,0:T(8,128)}, f32[16,256]{1,0:T(8,128)}, /*index=5*/f32[16,2048]{1,0:T(8,128)}, f32[8,128]{1,0:T(8,128)}) custom-call(bf16[1024,1024]{1,0:T(8,128)(2,1)} %get-tuple-element.34.qt, bf16[1024,1024]{1,0:T(8,128)(2,1)} %get-tuple-element.35.do_t, ...), custom_call_target="tpu_custom_call" | custom-call | tf_op jit(solution)/shard_map/tail/pallas_call | solution.py:1019
  152.1 5.0 %settle.1 = (bf16[512,2048]{1,0:T(8,128)(2,1)}, bf16[512,2048]{1,0:T(8,128)(2,1)}, f32[16,2048]{1,0:T(8,128)}, f32[16,256]{1,0:T(8,128)}, f32[16,256]{1,0:T(8,12...) custom-call(bf16[512,2048]{1,0:T(8,128)(2,1)} %get-tuple-element.47.refs_0_, bf16[512,2048]{1,0:T(8,128)(2,1)} %get-tuple-element.48.refs_1_, ...), custom_call_target="tpu_custom_call" | custom-call | tf_op jit(solution)/shard_map/settle/pallas_call | solution.py:1055
where the time goes:
time: 157 us
  Pallas kernels  156 us (99%)
    pallas_call x1, Pallas kernels, tail(): pl.pallas_call(tail_kernel, out_shape=[S(mine), S(mine), S((SHARE, DIM),...  95 us
    pallas_call x1, Pallas kernels, head(): pl.pallas_call(head_kernel, out_shape=[S(sq), S(sq), S(tall), S(wide), S(...  56.5 us
    pallas_call x1, Pallas kernels, settle(): pl.pallas_call(functools.partial(settle_kernel, len(large)), out_shape=[j...  5.01 us

commit v1 on v0

--- a/solution.py
+++ b/solution.py
@@ -569,7 +569,7 @@
         self.hops = {(a, hop): step(comm.pos, a, hop) for a in AXES for hop in (1, DUO, TRIO)}
         self.peer, self.core = comm.peer(), comm.core
         self.keep, self.give = tile_at(comm.core, SHARE), tile_at(1 - comm.core, SHARE)
-        self.drained = set()
+        self.drained, self.done = set(), []
 
     def slot(self, u):
         return COLOR[u], RANK[u] % SLOTS
@@ -630,8 +630,8 @@
             out, col = self.outs[TRIO], self.core * HALF + (u - 10) * LANES
         return out.at[:, pl.ds(pl.multiple_of(col, LANES), LANES)]
 
-    def kept(self, u):
-        return pltpu.make_async_copy(self.fin.at[u, self.keep], self.out(u), self.swap_sems.at[DUO + u])
+    def kept(self, u, turn):
+        return pltpu.make_async_copy(self.fin.at[u, self.keep], self.out(u), self.swap_sems.at[DUO + turn])
 
     def run(self, u, stage):
         if stage == 0:
@@ -642,7 +642,11 @@
             got = self.buf(u, DUO)
             self.fin[u] = self.view(u, DUO, 0)[...] + (got[0] + got[1] + got[DUO])
             self.copy(self.fin.at[u, self.give], self.out(u), (self.swap_sems.at[0], self.swap_sems.at[1]), self.peer).start()
-            self.kept(u).start()
+            turn = len(self.done) % DUO
+            if len(self.done) > 1:
+                self.kept(self.done[-DUO], turn).wait()
+            self.kept(u, turn).start()
+            self.done.append(u)
             return
         got = self.buf(u, phase)
         if stage % DUO:
@@ -671,8 +675,8 @@
         swaps = self.copy(half, half, (self.swap_sems.at[0], self.swap_sems.at[1]), self.peer)
         swaps.wait_send()
         swaps.wait_recv()
-        for u in range(N_UNITS):
-            self.kept(u).wait()
+        for turn in range(DUO):
+            self.kept(self.done[turn - DUO], turn).wait()
 
 
 def attend(heads, qt, do_t, k, kt, v, vt, cos, sin, o_row, ot, dq, dkt, dvt, s_scr, e_scr, p_scr, d_scr):
@@ -1025,7 +1029,7 @@
                         V((DUO, TOKENS, QB), f32), V((DUO, TOKENS, QB)), V((DUO, TOKENS, QB)), V((DUO, TOKENS, QB)), V(sq), V((PLACES, RING, RING, RING, CHIP, LANES), f32), V((TRIO, SLOTS, RING, RING, CHIP, LANES), f32),
                         V((TRIO, SLOTS, 6, RING, RING, SHARE, LANES), f32), V((TRIO, SLOTS, 6, RING, SHARE, LANES), f32), V((TRIO, SLOTS, TRIO, CHIP, LANES), f32), V((N_UNITS, CHIP, LANES), f32), V((TOKENS, ROWS)), V(mine), V((DUO * QKV, ROWS)), V(mine),
                         V((SUBS, DIM), f32), V((RING, SUBS, LANES), f32), V((RING, SUBS, LANES), f32), V((7, SUBS, LANES), f32), V((SHARE, SUBS, LANES), f32),
-                        D(9 * SLOTS), D(15 * SLOTS), D(DUO + N_UNITS), D(HEADS + RING), D(HEADS + RING), D(26)],
+                        D(9 * SLOTS), D(15 * SLOTS), D(RING), D(HEADS + RING), D(HEADS + RING), D(26)],
         compiler_params=pltpu.CompilerParams(collective_id=1, has_side_effects=True, vmem_limit_bytes=67043328),
         name='tail',
     )(qt, do_t, k, kt, v, vt, rt, dyc, wqk, wqkp, wvo, wvop, gain, hidden, dy, pos, cos, sin)

time: 157 us -> 157 us (level)
  no operation moved by 1% of the time
where the time goes in v1:
time: 157 us
  Pallas kernels  156 us (99%)
    pallas_call x1, Pallas kernels, tail(): pl.pallas_call(tail_kernel, out_shape=[S(mine), S(mine), S((SHARE, DIM),...  94.8 us
    pallas_call x1, Pallas kernels, head(): pl.pallas_call(head_kernel, out_shape=[S(sq), S(sq), S(tall), S(wide), S(...  56.5 us
    pallas_call x1, Pallas kernels, settle(): pl.pallas_call(functools.partial(settle_kernel, len(large)), out_shape=[j...  5.01 us

profile of v1, /device:TPU:1, one launch (start us, length us, event | category | flops | bytes accessed | tf_op | source)
XLA Modules:
  0.0 157.1 jit_solution(9453216171433798598)
XLA Ops:
  0.6 56.5 %head.1 = (bf16[1024,1024]{1,0:T(8,128)(2,1)}, bf16[1024,1024]{1,0:T(8,128)(2,1)}, bf16[1024,128]{1,0:T(8,128)(2,1)}, bf16[128,1024]{1,0:T(8,128)(2,1)}, bf16[10...) custom-call(bf16[512,2048]{1,0:T(8,128)(2,1)} %bitcast.10, ...), custom_call_target="tpu_custom_call" | custom-call | tf_op jit(solution)/shard_map/head/pallas_call | solution.py:457
  57.1 94.8 %tail.1 = (bf16[512,2048]{1,0:T(8,128)(2,1)}, bf16[512,2048]{1,0:T(8,128)(2,1)}, f32[16,2048]{1,0:T(8,128)}, f32[16,256]{1,0:T(8,128)}, f32[16,256]{1,0:T(8,128)}, /*index=5*/f32[16,2048]{1,0:T(8,128)}, f32[8,128]{1,0:T(8,128)}) custom-call(bf16[1024,1024]{1,0:T(8,128)(2,1)} %get-tuple-element.34.qt, bf16[1024,1024]{1,0:T(8,128)(2,1)} %get-tuple-element.35.do_t, ...), custom_call_target="tpu_custom_call" | custom-call | tf_op jit(solution)/shard_map/tail/pallas_call | solution.py:1023
  151.9 5.0 %settle.1 = (bf16[512,2048]{1,0:T(8,128)(2,1)}, bf16[512,2048]{1,0:T(8,128)(2,1)}, f32[16,2048]{1,0:T(8,128)}, f32[16,256]{1,0:T(8,128)}, f32[16,256]{1,0:T(8,12...) custom-call(bf16[512,2048]{1,0:T(8,128)(2,1)} %get-tuple-element.47.refs_0_, bf16[512,2048]{1,0:T(8,128)(2,1)} %get-tuple-element.48.refs_1_, ...), custom_call_target="tpu_custom_call" | custom-call | tf_op jit(solution)/shard_map/settle/pallas_call | solution.py:1059

commit v2 on v1

--- a/solution.py
+++ b/solution.py
@@ -781,13 +781,13 @@
         return [pltpu.make_async_remote_copy(src_ref=s, dst_ref=d, send_sem=trade_send.at[i], recv_sem=trade_recv.at[i], device_id=peer, device_id_type=MESH)
                 for s, d, i in ((ots.at[row], ots.at[row], g), (dqo.at[mine], dqp.at[mine], PAIRS + g))]
 
-    def gradient(place, count, left, right, mul):
+    def gradient(place, count, left, right, mul, steps=DUO):
         with scope('grad'):
-            @pl.loop(0, DUO)
+            @pl.loop(0, steps)
             def _(z):
-                g = mul(left[tile_at(z, HALF), :], right())
+                g = mul(left[tile_at(z, DIM // steps), :], right())
                 for i in range(count):
-                    part[place + i, tile_at(z, DUO)] = g[:, i * LANES:(i + 1) * LANES].reshape(DUO, RING, RING, CHIP, LANES)
+                    part[place + i, tile_at(z, RING // steps)] = g[:, i * LANES:(i + 1) * LANES].reshape(RING // steps, RING, RING, CHIP, LANES)
 
     attended, paired = [], []
     for g in range(PAIRS):
@@ -817,7 +817,7 @@
         for c in head_trades(g):
             c.start()
         at(attended)
-        gradient(DUO * g, DUO, rts, lambda: dqo[tile_at(g, PAIR), :], dot_nt)
+        gradient(DUO * g, DUO, rts, lambda: dqo[tile_at(g, PAIR), :], dot_nt, 1)
         at(paired)
 
     def beat(cost, *starts):

time: 157 us -> 157 us (level)
  no operation moved by 1% of the time
where the time goes in v2:
time: 157 us
  Pallas kernels  156 us (99%)
    pallas_call x1, Pallas kernels, tail(): pl.pallas_call(tail_kernel, out_shape=[S(mine), S(mine), S((SHARE, DIM),...  94.3 us
    pallas_call x1, Pallas kernels, head(): pl.pallas_call(head_kernel, out_shape=[S(sq), S(sq), S(tall), S(wide), S(...  56.5 us
    pallas_call x1, Pallas kernels, settle(): pl.pallas_call(functools.partial(settle_kernel, len(large)), out_shape=[j...  5.01 us

profile of v2, /device:TPU:1, one launch (start us, length us, event | category | flops | bytes accessed | tf_op | source)
XLA Modules:
  0.0 156.6 jit_solution(12339969656526208201)
XLA Ops:
  0.6 56.5 %head.1 = (bf16[1024,1024]{1,0:T(8,128)(2,1)}, bf16[1024,1024]{1,0:T(8,128)(2,1)}, bf16[1024,128]{1,0:T(8,128)(2,1)}, bf16[128,1024]{1,0:T(8,128)(2,1)}, bf16[10...) custom-call(bf16[512,2048]{1,0:T(8,128)(2,1)} %bitcast.10, ...), custom_call_target="tpu_custom_call" | custom-call | tf_op jit(solution)/shard_map/head/pallas_call | solution.py:457
  57.1 94.3 %tail.1 = (bf16[512,2048]{1,0:T(8,128)(2,1)}, bf16[512,2048]{1,0:T(8,128)(2,1)}, f32[16,2048]{1,0:T(8,128)}, f32[16,256]{1,0:T(8,128)}, f32[16,256]{1,0:T(8,128)}, /*index=5*/f32[16,2048]{1,0:T(8,128)}, f32[8,128]{1,0:T(8,128)}) custom-call(bf16[1024,1024]{1,0:T(8,128)(2,1)} %get-tuple-element.34.qt, bf16[1024,1024]{1,0:T(8,128)(2,1)} %get-tuple-element.35.do_t, ...), custom_call_target="tpu_custom_call" | custom-call | tf_op jit(solution)/shard_map/tail/pallas_call | solution.py:1023
  151.4 5.0 %settle.1 = (bf16[512,2048]{1,0:T(8,128)(2,1)}, bf16[512,2048]{1,0:T(8,128)(2,1)}, f32[16,2048]{1,0:T(8,128)}, f32[16,256]{1,0:T(8,128)}, f32[16,256]{1,0:T(8,12...) custom-call(bf16[512,2048]{1,0:T(8,128)(2,1)} %get-tuple-element.47.refs_0_, bf16[512,2048]{1,0:T(8,128)(2,1)} %get-tuple-element.48.refs_1_, ...), custom_call_target="tpu_custom_call" | custom-call | tf_op jit(solution)/shard_map/settle/pallas_call | solution.py:1059

commit v3 on v2

--- a/solution.py
+++ b/solution.py
@@ -791,8 +791,8 @@
 
     attended, paired = [], []
     for g in range(PAIRS):
-        attended.append(after(5.1))
-        plan.now += 1.5
+        attended.append(after(5.15))
+        plan.now += 1.4
         plan.start(DUO * g)
         plan.start(DUO * g + 1)
         paired.append(plan.due())

time: 157 us -> 154 us (0.981)
  Pallas kernels: 156 us -> 153 us
    pallas_call x1, Pallas kernels: 94.3 us -> 91.7 us  [tail(): pl.pallas_call(tail_kernel, out_shape=[S(mine), S(mine), S((SHARE, DIM),...]
where the time goes in v3:
time: 154 us
  Pallas kernels  153 us (99%)
    pallas_call x1, Pallas kernels, tail(): pl.pallas_call(tail_kernel, out_shape=[S(mine), S(mine), S((SHARE, DIM),...  91.7 us
    pallas_call x1, Pallas kernels, head(): pl.pallas_call(head_kernel, out_shape=[S(sq), S(sq), S(tall), S(wide), S(...  56.5 us
    pallas_call x1, Pallas kernels, settle(): pl.pallas_call(functools.partial(settle_kernel, len(large)), out_shape=[j...  5.01 us

profile of v3, /device:TPU:1, one launch (start us, length us, event | category | flops | bytes accessed | tf_op | source)
XLA Modules:
  0.0 154.0 jit_solution(2268781361661529447)
XLA Ops:
  0.6 56.5 %head.1 = (bf16[1024,1024]{1,0:T(8,128)(2,1)}, bf16[1024,1024]{1,0:T(8,128)(2,1)}, bf16[1024,128]{1,0:T(8,128)(2,1)}, bf16[128,1024]{1,0:T(8,128)(2,1)}, bf16[10...) custom-call(bf16[512,2048]{1,0:T(8,128)(2,1)} %bitcast.10, ...), custom_call_target="tpu_custom_call" | custom-call | tf_op jit(solution)/shard_map/head/pallas_call | solution.py:457
  57.1 91.7 %tail.1 = (bf16[512,2048]{1,0:T(8,128)(2,1)}, bf16[512,2048]{1,0:T(8,128)(2,1)}, f32[16,2048]{1,0:T(8,128)}, f32[16,256]{1,0:T(8,128)}, f32[16,256]{1,0:T(8,128)}, /*index=5*/f32[16,2048]{1,0:T(8,128)}, f32[8,128]{1,0:T(8,128)}) custom-call(bf16[1024,1024]{1,0:T(8,128)(2,1)} %get-tuple-element.34.qt, bf16[1024,1024]{1,0:T(8,128)(2,1)} %get-tuple-element.35.do_t, ...), custom_call_target="tpu_custom_call" | custom-call | tf_op jit(solution)/shard_map/tail/pallas_call | solution.py:1023
  148.8 5.0 %settle.1 = (bf16[512,2048]{1,0:T(8,128)(2,1)}, bf16[512,2048]{1,0:T(8,128)(2,1)}, f32[16,2048]{1,0:T(8,128)}, f32[16,256]{1,0:T(8,128)}, f32[16,256]{1,0:T(8,12...) custom-call(bf16[512,2048]{1,0:T(8,128)(2,1)} %get-tuple-element.47.refs_0_, bf16[512,2048]{1,0:T(8,128)(2,1)} %get-tuple-element.48.refs_1_, ...), custom_call_target="tpu_custom_call" | custom-call | tf_op jit(solution)/shard_map/settle/pallas_call | solution.py:1059
